TPU v7x, 32 devices: a whole 2x2x4 slice. The times are simulated.
32 devices in a mesh: rows: 4 (over y, x), cols: 8 (over z, core).
Axes of the slice: x: 2, y: 2, z: 4, core: 2. Of those that a mesh axis runs over, the one named last changes fastest.
Arguments:
- factor_u: float32 [4, 2048, 128], P('rows', 'cols'), may hold values from -2 to 2
- factor_v: float32 [8, 512, 128], P('cols', 'rows'), may hold values from -2 to 2
- values: bfloat16 [4, 8, 8, 256, 256], P('rows', 'cols'), may hold values from -6 to 6
- mask_words: int32 [4, 8, 8, 16, 256], P('rows', 'cols'), may hold values from 0 to 65535, as said below
- tile_cols: int32 [4, 8, 8], P('rows', 'cols'), may hold values from 0 to 1
Outputs:
- new_u: float32 [4, 2048, 128], P('rows', 'cols')
- new_v: float32 [8, 512, 128], P('cols', 'rows')
- loss: float32 [], replicated
Inputs may be any that keep to these rules, and one draw needn't show every extreme that they name: `mask_words`: bit b of word w of a slot marks the entry in row 16 w + b of the tile.
All inputs are finite; a program needn't handle non-finite values.
Results may differ from a plain program's by a relative error of at most 0.02.
Values may be sent and summed in bfloat16 or wider, within the bound.
A program may use at most 64 MiB of HBM per device.

v0:
```python
import jax
import jax.numpy as jnp
from jax import lax
from jax.sharding import PartitionSpec as P

step_rate = 0.01
ridge_weight = 0.1


def decode(mask_bits):
    shifts = jnp.arange(16, dtype=jnp.int32)
    bit_values = jnp.bitwise_and(
        jnp.right_shift(mask_bits[:, :, None, :], shifts[None, None, :, None]), 1
    )
    return bit_values.reshape(
        mask_bits.shape[0], mask_bits.shape[1] * 16, mask_bits.shape[2]
    ).astype(jnp.float32)


def slot_terms(left_rows, tile_values, mask_bits, column_ids, right_tiles):
    observed = decode(mask_bits)
    right_rows = jnp.take(right_tiles, column_ids, axis=0)
    predicted = jnp.einsum(
        "sik,sjk->sij", left_rows, right_rows, preferred_element_type=jnp.float32
    )
    residual = observed * (predicted - tile_values.astype(jnp.float32))
    squares = 0.5 * jnp.sum(residual * residual)
    resid_low = residual.astype(jnp.bfloat16)
    grad_rows = jnp.einsum(
        "sij,sjk->sik", resid_low, right_rows, preferred_element_type=jnp.float32
    )
    first = grad_rows.reshape(-1, left_rows.shape[2])
    grad_cols = jnp.einsum("sij,sik->sjk", resid_low, left_rows, preferred_element_type=jnp.float32)
    selector = (
        column_ids[:, None] == jnp.arange(right_tiles.shape[0], dtype=jnp.int32)[None, :]
    ).astype(jnp.float32)
    col_sums = jnp.einsum(
        "sq,sx->qx",
        selector,
        grad_cols.reshape(grad_cols.shape[0], -1),
        precision=lax.Precision.HIGHEST,
        preferred_element_type=jnp.float32,
    )
    return (first, col_sums, squares)


def band_terms(left_tiles, tile_values, mask_bits, column_ids, right_tiles):
    tile_count = left_tiles.shape[0]
    row_parts = []
    col_total = jnp.zeros(
        (right_tiles.shape[0], right_tiles.shape[1] * right_tiles.shape[2]), jnp.float32
    )
    square_total = jnp.zeros((), jnp.float32)
    for block_start in range(0, tile_count, 8):
        block_len = min(8, tile_count - block_start)
        block_end = block_start + block_len
        first, col_sums, squares = slot_terms(
            left_tiles[block_start:block_end],
            tile_values[block_start:block_end],
            mask_bits[block_start:block_end],
            column_ids[block_start:block_end],
            right_tiles,
        )
        row_parts.append(first)
        col_total = col_total + col_sums
        square_total = square_total + squares
    return (jnp.concatenate(row_parts, axis=0), col_total, square_total)


def per_device(factor_u, factor_v, values, mask_words, tile_cols):
    owned_left = factor_u[0]
    owned_right = factor_v[0]
    tile_values = values[0, 0]
    mask_bits = mask_words[0, 0]
    column_ids = tile_cols[0, 0]
    tile_size = tile_values.shape[-1]
    factor_rank = owned_left.shape[-1]
    slot_count = tile_values.shape[0]
    v_band = lax.all_gather(owned_right.astype(jnp.bfloat16), "rows", axis=0, tiled=True)
    right_tiles = v_band.reshape(-1, tile_size, factor_rank)
    u_low = owned_left.astype(jnp.bfloat16)
    u_band = lax.all_gather(u_low, "cols", axis=0, tiled=True)
    first_rows, col_total, square_total = band_terms(
        u_band.reshape(-1, tile_size, factor_rank), tile_values, mask_bits, column_ids, right_tiles
    )
    grad_u = lax.psum_scatter(
        first_rows.astype(jnp.bfloat16), "cols", scatter_dimension=0, tiled=True
    ).astype(jnp.float32)
    grad_v = lax.psum_scatter(
        col_total.reshape(-1, factor_rank).astype(jnp.bfloat16),
        "rows",
        scatter_dimension=0,
        tiled=True,
    ).astype(jnp.float32)
    local_sum = square_total + 0.5 * ridge_weight * (
        jnp.sum(owned_left * owned_left) + jnp.sum(owned_right * owned_right)
    )
    total = lax.psum(local_sum, ("rows", "cols"))
    entries = lax.axis_size("rows") * lax.axis_size("cols") * slot_count * tile_size * tile_size
    new_left = owned_left - step_rate * (grad_u + ridge_weight * owned_left)
    new_right = owned_right - step_rate * (grad_v + ridge_weight * owned_right)
    return (new_left[None], new_right[None], total / entries)


def solution(mesh):
    in_specs = (
        P("rows", "cols", None),
        P("cols", "rows", None),
        P("rows", "cols", None, None, None),
        P("rows", "cols", None, None, None),
        P("rows", "cols", None),
    )
    out_specs = (P("rows", "cols", None), P("cols", "rows", None), P())
    return jax.shard_map(
        per_device, mesh=mesh, in_specs=in_specs, out_specs=out_specs, check_vma=False
    )
```

profile of v0, /device:TPU:0, one launch (start us, length us, event | category | flops | bytes accessed | tf_op | source)
XLA Modules:
  0.0 158.1 jit_solution(17109116347716289053)
XLA Ops:
  7.2 0.0 reduce-scatter.5.cloned.1.call-start
  7.2 0.7 fusion.14
  7.9 0.7 compare_and_fusion
  8.5 0.8 bitcast_convert_fusion.1
  9.4 9.9 %all_gather.6 = bf16[512,128]{1,0:T(8,128)(2,1)S(1)} all-gather(bf16[128,128]{1,0:T(8,128)(2,1)S(1)} %bitcast_convert_fusion.1), channel_id=1, replica_groups=mesh['rows'=4,'cols'=8] {'rows'}, dimensions={0}, use_global_device_ids=true | all-gather | bytes 163840 | tf_op jit(solution)/shard_map/all_gather | solution.py:79
  19.3 0.9 bitcast_convert_fusion
  20.2 16.0 %all_gather.7 = bf16[2048,128]{1,0:T(8,128)(2,1)} all-gather(bf16[256,128]{1,0:T(8,128)(2,1)S(1)} %bitcast_convert_fusion), channel_id=1, replica_groups=mesh['rows'=4,'cols'=8] {'cols'}, dimensions={0}, use_global_device_ids=true | all-gather | bytes 589824 | tf_op jit(solution)/shard_map/all_gather | solution.py:82
  36.3 2.4 %shift_right_arithmetic.23 = s32[8,16,16,256]{3,2,1,0:T(8,128)} broadcast(s32[8,16,256]{2,1,0:T(8,128)} %bitcast.64), dimensions={0,1,3} | broadcast | bytes 2228224 | tf_op jit(solution)/shard_map/shift_right_arithmetic | solution.py:13
  38.7 1.9 %copy.11 = s32[8,256,256]{1,2,0:T(8,128)S(1)} copy(s32[8,256,256]{2,1,0:T(8,128)} %bitcast.59) | data formatting | bytes 4194304 | tf_op jit(solution)/shard_map/shift_right_arithmetic | solution.py:13
  40.6 2.3 %copy.12 = bf16[1,1,8,256,256]{3,4,2,1,0:T(8,128)(2,1)} copy(bf16[1,1,8,256,256]{4,3,2,1,0:T(8,128)(2,1)} %param.7) | data formatting | bytes 2097152 | tf_op args[2]
  42.9 0.1 shift_right_arithmetic.26
  43.0 1.4 gather_fusion
  44.4 0.0 copy-start
  44.4 3.0 %multiply_reduce_fusion = (f32[]{:T(128)}, bf16[8,256,256]{1,2,0:T(8,128)(2,1)S(1)}) fusion(bf16[1,1,8,256,256]{3,4,2,1,0:T(8,128)(2,1)} %copy.12, bf16[8,256,128]{2,1,0:T(8,128)(2,1)} %bitcast.60, bf16[8,256,128]{2,1,0:T(8,128)(2,1)} %gather_fusion, pred[8]{0:T(512)(128)(4,1)S(1)} %compare_and_fusion, s32[8,256,256]{1,2,0:T(8,128)S(1)} %copy.11, ...), kind=kOutput, calls=%fused_computation.4 | convolution fusion | flops 139198464 | bytes 5243916 | tf_op jit(solution)/shard_map/sik,sjk->sij/dot_general | solution.py:23
  47.5 0.0 copy-start.4
  47.5 0.0 copy-done
  47.5 0.0 copy-start.1
  47.5 0.4 convolution_bitcast_fusion
  47.9 0.2 copy-done.4
  48.1 0.0 copy-start.3
  48.1 0.0 copy-start.2
  48.1 1.2 convolution_convert_fusion
  49.4 0.8 convert_element_type.47
  50.1 0.0 reduce-scatter.5.cloned.1.call-update
  50.1 0.0 reduce-scatter.3.cloned.1.call-start
  50.2 0.0 copy-done.1
  50.2 1.3 convolution_convert_fusion.1
  51.5 0.0 reduce-scatter.3.cloned.1.call-update
  52.2 22.4 %reduce-scatter.5.cloned.1.call-done = bf16[128,128]{1,0:T(8,128)(2,1)} async-done(((bf16[512,128]{1,0:T(8,128)(2,1)}), bf16[128,128]{1,0:T(8,128)(2,1)}) %reduce-scatter.5.cloned.1.call-update) | async-done | bytes 32784 | tf_op jit(solution)/shard_map/reduce_scatter | solution.py:89
  74.6 0.0 copy-done.3
  74.6 2.1 %fusion.12 = (f32[]{:T(128)}, f32[1,128,128]{2,1,0:T(8,128)}) fusion(f32[1,128,128]{2,1,0:T(8,128)S(1)} %copy-done.3, bf16[128,128]{1,0:T(8,128)(2,1)} %reduce-scatter.5.cloned.1.call-done), kind=kLoop, calls=%fused_computation.27 | loop fusion | flops 114687 | bytes 163844 | tf_op jit(solution)/shard_map/reduce_sum | solution.py:96
  76.7 31.6 %reduce-scatter.3.cloned.1.call-done = bf16[256,128]{1,0:T(8,128)(2,1)} async-done(((bf16[2048,128]{1,0:T(8,128)(2,1)}), bf16[256,128]{1,0:T(8,128)(2,1)}) %reduce-scatter.3.cloned.1.call-update) | async-done | bytes 65552 | tf_op jit(solution)/shard_map/reduce_scatter | solution.py:86
  108.3 0.0 copy-done.2
  108.3 2.1 %fusion.8 = (f32[]{:T(128)}, f32[1,256,128]{2,1,0:T(8,128)}) fusion(f32[1,256,128]{2,1,0:T(8,128)S(1)} %copy-done.2, bf16[256,128]{1,0:T(8,128)(2,1)} %reduce-scatter.3.cloned.1.call-done), kind=kLoop, calls=%fused_computation.19 | loop fusion | flops 229375 | bytes 327684 | tf_op jit(solution)/shard_map/reduce_sum | solution.py:96
  111.8 37.7 %psum.7 = f32[]{:T(128)} all-reduce(f32[]{:T(128)S(6)} %add.38), channel_id=1, replica_groups=mesh['rows'=4,'cols'=8] {'rows','cols'}, use_global_device_ids=true, to_apply=%region_5.6 | all-reduce | flops 1 | bytes 8 | tf_op jit(solution)/shard_map/psum | solution.py:98
  (2 shorter events, 0.0 us)
Async XLA Ops:
  7.2 67.5 %reduce-scatter.5.cloned.1.call-start = ((), (), s32[]{:S(2)}) async-start(), calls=%async_computation.3 | async-start | bytes 163840 | tf_op jit(solution)/shard_map/reduce_scatter | solution.py:89
  44.4 3.0 %copy-start = (bf16[2048,128]{1,0:T(8,128)(2,1)S(1)}, bf16[2048,128]{1,0:T(8,128)(2,1)}, u32[]{:S(2)}) copy-start(bf16[2048,128]{1,0:T(8,128)(2,1)} %all_gather.7) | copy-start | bytes 1572868
  47.5 0.7 copy-start.4
  47.5 2.7 %copy-start.1 = (bf16[8,256,128]{2,1,0:T(8,128)(2,1)S(1)}, bf16[8,256,128]{2,1,0:T(8,128)(2,1)}, u32[]{:S(2)}) copy-start(bf16[8,256,128]{2,1,0:T(8,128)(2,1)} %gather_fusion) | copy-start | bytes 1572868
  48.1 26.5 %copy-start.3 = (f32[1,128,128]{2,1,0:T(8,128)S(1)}, f32[1,128,128]{2,1,0:T(8,128)}, u32[]{:S(2)}) copy-start(f32[1,128,128]{2,1,0:T(8,128)} %param.6) | copy-start | bytes 196612
  48.1 60.2 %copy-start.2 = (f32[1,256,128]{2,1,0:T(8,128)S(1)}, f32[1,256,128]{2,1,0:T(8,128)}, u32[]{:S(2)}) copy-start(f32[1,256,128]{2,1,0:T(8,128)} %param.5) | copy-start | bytes 393220
  50.1 58.2 %reduce-scatter.3.cloned.1.call-start = ((), (), s32[]{:S(2)}) async-start(), calls=%async_computation.2 | async-start | bytes 589824 | tf_op jit(solution)/shard_map/reduce_scatter | solution.py:86
Sparse Core Ops, SparseCore 0:
  50.3 24.3 reduce-scatter.4
  76.9 31.3 reduce-scatter.2
where the time goes:
time: 159 us; the launch traced here: 158 us
  blocking collectives  63.6 us (40%)
  waiting for transfers between devices  54.1 us (34%)
  between operations  17.8 us (11%)
  local copies, waits for them, and re-layouts  9.13 us (6%)
  other arithmetic  7.27 us (5%)
  matrix products  6 us (4%)
    psum x1, blocking collectives, per_device(): total = lax.psum(local_sum, ('rows', 'cols'))  37.7 us
    reduce_scatter x1, waiting for transfers between devices, per_device(): lax.psum_scatter(first_rows.astype(jnp.bfloat16), 'cols', scatter_dimensi...  31.6 us
    reduce_scatter x1, waiting for transfers between devices, per_device(): lax.psum_scatter(col_total.reshape(-1, factor_rank).astype(jnp.bfloat16),...  22.4 us
    all_gather x1, blocking collectives, per_device(): u_band = lax.all_gather(u_low, 'cols', axis=0, tiled=True)  16 us
    all_gather x1, blocking collectives, per_device(): lax.all_gather(owned_right.astype(jnp.bfloat16), 'rows', axis=0, tiled=True)  9.93 us
    shift_right_arithmetic x4, local copies, waits for them, and re-layouts, decode(): jnp.right_shift(mask_bits[:, :, None, :], shifts[None, None, :, None])  4.43 us
  transfers between devices with their start and end apart: 2, of which 2 were waited for; matrix products, arithmetic and copies ran while one was open for 2% of the time, Pallas kernels for 0%

commit v1 on v0

v1 whole, which is shorter than its diff:
```python
import functools

import jax
import jax.numpy as jnp
from jax import lax
from jax.experimental import pallas as pl
from jax.experimental.pallas import tpu as pltpu
from jax.sharding import PartitionSpec as P

step_rate = 0.01
ridge_weight = 0.1
MESH = pl.DeviceIdType.MESH
NT = (((1,), (1,)), ((), ()))
TN = (((0,), (0,)), ((), ()))
WORD = 16


def loop(start, stop, body):
    if stop - start <= 8:
        for i in range(start, stop):
            body(i)
    else:
        lax.fori_loop(start, stop, lambda i, z: (body(i), z)[1], 0)


def fold(x):
    return jnp.sum(x.reshape(x.shape[0] // 8, 8, x.shape[1]), axis=0)


def kernel(
    n_r, n_c, entries,
    u_hbm, v_hbm, val_hbm, mask_hbm, tc_ref,
    nu_ref, nv_ref, loss_ref,
    uf, vf, vals, masks, ub, vb, keep, xsend, pbuf, rsend, rbuf,
    acc, vsend, vrecv, sq, lrow, lcol,
    ld_sem, vg_s, vg_r, ug_s, ug_r, ud_s, ud_r, pd_s, pd_r, pr_s, pr_r,
    vr_s, vr_r, lr_s, lr_r, lc_s, lc_r,
):
    n_q = n_c // 2
    r = lax.axis_index("rows")
    c = lax.axis_index("cols")
    q = c // 2
    a = c % 2
    pc = 2 * q + 1 - a
    tile = vals.shape[1]
    own_v = vf.shape[0]
    per_tile = tile // own_v

    ld_u = pltpu.make_async_copy(u_hbm.at[0], uf, ld_sem.at[0])
    ld_v = pltpu.make_async_copy(v_hbm.at[0], vf, ld_sem.at[1])
    ld_m = pltpu.make_async_copy(mask_hbm.at[0, 0], masks, ld_sem.at[2])
    ld_x = pltpu.make_async_copy(val_hbm.at[0, 0], vals, ld_sem.at[3])
    ld_v.start()
    ld_u.start()
    ld_m.start()
    ld_x.start()

    bar = pltpu.get_barrier_semaphore()

    def greet_row(d):
        pl.semaphore_signal(bar, inc=1, device_id=((r + d) % n_r, c), device_id_type=MESH)

    def greet_col(d):
        pl.semaphore_signal(bar, inc=1, device_id=(r, (c + d) % n_c), device_id_type=MESH)

    loop(1, n_r, greet_row)
    loop(1, n_c, greet_col)

    ld_v.wait()
    vb[r // per_tile, pl.ds(pl.multiple_of((r % per_tile) * own_v, own_v), own_v)] = vf[...].astype(jnp.bfloat16)
    ld_u.wait()
    ub[c] = uf[...].astype(jnp.bfloat16)
    sq[...] = jnp.zeros_like(sq)
    acc[...] = jnp.zeros_like(acc)
    penalty = fold(uf[...] * uf[...]) + fold(vf[...] * vf[...])

    pl.semaphore_wait(bar, n_r + n_c - 2)

    def chunk(i):
        return vb.at[i // per_tile, pl.ds(pl.multiple_of((i % per_tile) * own_v, own_v), own_v)]

    def rdma(src, dst, s, g, dev):
        return pltpu.make_async_remote_copy(
            src_ref=src, dst_ref=dst, send_sem=s, recv_sem=g, device_id=dev, device_id_type=MESH
        )

    def vg(d):
        return rdma(chunk(r), chunk(r), vg_s.at[d], vg_r.at[d], ((r + d) % n_r, c))

    def vg_in(d):
        src = (r + n_r - d) % n_r
        return rdma(chunk(src), chunk(src), vg_s.at[d], vg_r.at[d], ((r + d) % n_r, c))

    def chip(d):
        return (q + n_q - d) % n_q

    def ug(d):
        return rdma(ub.at[c], ub.at[c], ug_s.at[d], ug_r.at[d], (r, 2 * ((q + d) % n_q) + a))

    def ug_in(d):
        s = 2 * chip(d) + a
        return rdma(ub.at[s], ub.at[s], ug_s.at[d], ug_r.at[d], (r, 2 * ((q + d) % n_q) + a))

    def ud(d):
        s = 2 * chip(d) + a
        return rdma(ub.at[s], ub.at[s], ud_s.at[d], ud_r.at[d], (r, pc))

    def ud_in(d):
        s = 2 * chip(d) + 1 - a
        return rdma(ub.at[s], ub.at[s], ud_s.at[d], ud_r.at[d], (r, pc))

    def pd(d):
        return rdma(xsend.at[d], pbuf.at[d], pd_s.at[d], pd_r.at[d], (r, pc))

    def pr(d):
        return rdma(rsend.at[d], rbuf.at[d], pr_s.at[d], pr_r.at[d], (r, 2 * chip(d) + a))

    def vr(d):
        return rdma(vsend.at[(r + d) % n_r], vrecv.at[d], vr_s.at[d], vr_r.at[d], ((r + d) % n_r, c))

    def lr(d):
        return rdma(lrow.at[r], lrow.at[r], lr_s.at[d], lr_r.at[d], ((r + d) % n_r, c))

    def lr_in(d):
        src = (r + n_r - d) % n_r
        return rdma(lrow.at[src], lrow.at[src], lr_s.at[d], lr_r.at[d], ((r + d) % n_r, c))

    def lc(d):
        return rdma(lcol.at[c], lcol.at[c], lc_s.at[d], lc_r.at[d], (r, (c + d) % n_c))

    def lc_in(d):
        src = (c + n_c - d) % n_c
        return rdma(lcol.at[src], lcol.at[src], lc_s.at[d], lc_r.at[d], (r, (c + d) % n_c))

    loop(1, n_r, lambda d: vg(d).start())
    ud(0).start()
    loop(1, n_q, lambda d: ug(d).start())

    ld_m.wait()
    ld_x.wait()
    loop(1, n_r, lambda d: vg_in(d).wait_recv())

    bits = lax.shift_left(jnp.int32(1), lax.broadcasted_iota(jnp.int32, (1, WORD, tile), 1))

    def slot(s, put):
        left = ub[s]
        which = tc_ref[0, 0, s]
        right = vb[which]
        predicted = lax.dot_general(left, right, NT, preferred_element_type=jnp.float32)
        words = masks[s]
        seen = (jnp.broadcast_to(words[:, None, :], (tile // WORD, WORD, tile)) & bits).reshape(tile, tile) != 0
        residual = jnp.where(seen, predicted - vals[s].astype(jnp.float32), 0.0)
        low = residual.astype(jnp.bfloat16)
        put(jnp.dot(low, right, preferred_element_type=jnp.float32))
        sq[...] += fold(residual * residual)
        cols_t = lax.dot_general(left, low, TN, preferred_element_type=jnp.float32)
        for t in range(acc.shape[0]):
            acc[t] += cols_t * (which == t).astype(jnp.float32)

    def put_keep(d):
        def put(x):
            keep[d] = x
        return put

    def put_send(d):
        def put(x):
            xsend[d] = x.astype(jnp.bfloat16)
        return put

    def stage_c(d):
        pd(d).wait_recv()
        rsend[d] = (keep[d] + pbuf[d].astype(jnp.float32)).astype(jnp.bfloat16)
        pr(d).start()

    def stage_a(d):
        ug_in(d).wait_recv()
        ud(d).start()
        slot(2 * chip(d) + a, put_keep(d))

    def stage_b(d):
        ud_in(d).wait_recv()
        slot(2 * chip(d) + 1 - a, put_send(d))
        pd(d).start()

    slot(c, put_keep(0))
    stage_b(0)
    stage_a(1)
    stage_b(1)

    def step(d):
        stage_a(d)
        stage_c(d - 1)
        stage_b(d)

    loop(2, n_q, step)

    half = sq.shape[1] // 2
    lrow[r] = 0.5 * (sq[:, :half] + sq[:, half:]) + 0.5 * ridge_weight * penalty

    for t in range(acc.shape[0]):
        whole = acc[t].T.astype(jnp.bfloat16)
        for h in range(per_tile):
            vsend[t * per_tile + h] = whole[h * own_v:(h + 1) * own_v]
    loop(1, n_r, lambda d: lr(d).start())
    loop(1, n_r, lambda d: vr(d).start())
    stage_c(n_q - 1)

    loop(1, n_r, lambda d: lr_in(d).wait_recv())
    total = lrow[0]
    for i in range(1, n_r):
        total = total + lrow[i]
    lcol[c] = total
    pd(0).wait_recv()
    keep[0] = keep[0] + pbuf[0].astype(jnp.float32)
    loop(1, n_c, lambda d: lc(d).start())

    def add_v(d):
        vr(d).wait_recv()
        vf_sum[...] += vrecv[d].astype(jnp.float32)

    vf_sum = nv_ref.at[0]
    vf_sum[...] = vsend[r].astype(jnp.float32)
    loop(1, n_r, add_v)
    vf_sum[...] = vf[...] - step_rate * (vf_sum[...] + ridge_weight * vf[...])

    def add_u(d):
        pr(d).wait_recv()
        keep[0] += rbuf[d].astype(jnp.float32)

    loop(1, n_q, add_u)
    nu_ref[0] = uf[...] - step_rate * (keep[0] + ridge_weight * uf[...])

    loop(1, n_c, lambda d: lc_in(d).wait_recv())
    total = lcol[0]
    for i in range(1, n_c):
        total = total + lcol[i]
    loss_ref[...] = jnp.sum(jnp.sum(total, axis=1, keepdims=True), axis=0, keepdims=True) / entries

    def drain_q(d):
        ud(d).wait_send()
        pd(d).wait_send()

    def drain_q1(d):
        ug(d).wait_send()
        pr(d).wait_send()

    def drain_r(d):
        vg(d).wait_send()
        vr(d).wait_send()
        lr(d).wait_send()

    loop(0, n_q, drain_q)
    loop(1, n_q, drain_q1)
    loop(1, n_r, drain_r)
    loop(1, n_c, lambda d: lc(d).wait_send())


def per_device(n_r, n_c, factor_u, factor_v, values, mask_words, tile_cols):
    _, own_u, rank = factor_u.shape
    own_v = factor_v.shape[1]
    slots, tile = values.shape[2], values.shape[3]
    n_q = n_c // 2
    entries = n_r * n_c * slots * tile * tile
    col_tiles = n_r * own_v // tile
    dma = pltpu.SemaphoreType.DMA
    bf, f32 = jnp.bfloat16, jnp.float32
    anym = pl.BlockSpec(memory_space=pl.ANY)
    vm = pl.BlockSpec(memory_space=pltpu.VMEM)
    new_u, new_v, loss = pl.pallas_call(
        functools.partial(kernel, n_r, n_c, float(entries)),
        out_shape=(
            jax.ShapeDtypeStruct(factor_u.shape, f32),
            jax.ShapeDtypeStruct(factor_v.shape, f32),
            jax.ShapeDtypeStruct((1, 1), f32),
        ),
        in_specs=[anym, anym, anym, anym, pl.BlockSpec(memory_space=pltpu.SMEM)],
        out_specs=(vm, vm, vm),
        scratch_shapes=[
            pltpu.VMEM((own_u, rank), f32),
            pltpu.VMEM((own_v, rank), f32),
            pltpu.VMEM(values.shape[2:], bf),
            pltpu.VMEM(mask_words.shape[2:], jnp.int32),
            pltpu.VMEM((n_c, own_u, rank), bf),
            pltpu.VMEM((col_tiles, tile, rank), bf),
            pltpu.VMEM((n_q, own_u, rank), f32),
            pltpu.VMEM((n_q, own_u, rank), bf),
            pltpu.VMEM((n_q, own_u, rank), bf),
            pltpu.VMEM((n_q, own_u, rank), bf),
            pltpu.VMEM((n_q, own_u, rank), bf),
            pltpu.VMEM((col_tiles, rank, tile), f32),
            pltpu.VMEM((n_r, own_v, rank), bf),
            pltpu.VMEM((n_r, own_v, rank), bf),
            pltpu.VMEM((8, tile), f32),
            pltpu.VMEM((n_r, 8, tile // 2), f32),
            pltpu.VMEM((n_c, 8, tile // 2), f32),
            dma((4,)),
            dma((n_r,)), dma((n_r,)),
            dma((n_q,)), dma((n_q,)),
            dma((n_q,)), dma((n_q,)),
            dma((n_q,)), dma((n_q,)),
            dma((n_q,)), dma((n_q,)),
            dma((n_r,)), dma((n_r,)),
            dma((n_r,)), dma((n_r,)),
            dma((n_c,)), dma((n_c,)),
        ],
        compiler_params=pltpu.CompilerParams(collective_id=0, has_side_effects=True),
    )(factor_u, factor_v, values, mask_words, tile_cols)
    return new_u, new_v, loss[0, 0]


def solution(mesh):
    n_r, n_c = mesh.shape["rows"], mesh.shape["cols"]
    in_specs = (
        P("rows", "cols", None),
        P("cols", "rows", None),
        P("rows", "cols", None, None, None),
        P("rows", "cols", None, None, None),
        P("rows", "cols", None),
    )
    out_specs = (P("rows", "cols", None), P("cols", "rows", None), P())
    return jax.shard_map(
        functools.partial(per_device, n_r, n_c),
        mesh=mesh, in_specs=in_specs, out_specs=out_specs, check_vma=False,
    )
```

time: 159 us -> 30.1 us (0.19)
  blocking collectives: 63.6 us -> 0 us
  waiting for transfers between devices: 54.1 us -> 0 us
  Pallas kernels: 0 us -> 25.4 us
  between operations: 17.8 us -> 2.34 us
  other arithmetic: 7.27 us -> 0 us
  local copies, waits for them, and re-layouts: 9.13 us -> 2.23 us
  matrix products: 6 us -> 0 us
    reduce_scatter x2 -> x0, waiting for transfers between devices: 54.1 us -> none  [the longest x1 31.6 us: per_device(): lax.psum_scatter(first_rows.astype(jnp.bfloat16), 'cols', scatter_dimensi...]
    psum x1 -> x0, blocking collectives: 37.7 us -> none  [per_device(): total = lax.psum(local_sum, ('rows', 'cols'))]
    all_gather x2 -> x0, blocking collectives: 26 us -> none  [the longest x1 16 us: per_device(): u_band = lax.all_gather(u_low, 'cols', axis=0, tiled=True)]
    pallas_call x0 -> x1, Pallas kernels: none -> 25.4 us  [per_device(): pl.pallas_call(functools.partial(kernel, n_r, n_c, float(entries)), out_s...]
    dot_general x4 -> x0, matrix products: 6 us -> none  [the longest x1 3.03 us: slot_terms(): jnp.einsum('sik,sjk->sij', left_rows, right_rows, preferred_element_type=...]
    shift_right_arithmetic x4 -> x0, local copies, waits for them, and re-layouts: 4.43 us -> none  [decode(): jnp.right_shift(mask_bits[:, :, None, :], shifts[None, None, :, None])]
    reduce_sum x2 -> x0, other arithmetic: 4.19 us -> none  [the longest x1 2.12 us: per_device(): jnp.sum(owned_left * owned_left) + jnp.sum(owned_right * owned_right)]
    convert_element_type x2 -> x0, other arithmetic: 1.76 us -> none  [the longest x1 0.91 us: per_device(): u_low = owned_left.astype(jnp.bfloat16)]
  transfers between devices with their start and end apart: 2 -> 0, of which waited for: 2 -> 0; matrix products, arithmetic and copies ran while one was open for 2% -> 0% of each run, Pallas kernels for 0% -> 0%
where the time goes in v1:
time: 30.1 us; the launch traced here: 29.9 us
  Pallas kernels  25.4 us (84%)
  between operations  2.34 us (8%)
  local copies, waits for them, and re-layouts  2.23 us (7%)
    pallas_call x1, Pallas kernels, per_device(): pl.pallas_call(functools.partial(kernel, n_r, n_c, float(entries)), out_s...  25.4 us
    unnamed x4, local copies, waits for them, and re-layouts  2.23 us

profile of v1, /device:TPU:0, one launch (start us, length us, event | category | flops | bytes accessed | tf_op | source)
XLA Modules:
  0.0 29.9 jit_solution(18335342223918585888)
XLA Ops:
  0.6 25.4 %shard_map.76 = (f32[1,256,128]{2,1,0:T(8,128)}, f32[1,128,128]{2,1,0:T(8,128)}, f32[1,1]{1,0:T(1,128)}) custom-call(f32[1,256,128]{2,1,0:T(8,128)} %u_hbm.1, f32[1,128,128]{2,1,0:T(8,128)} %v_hbm.1, bf16[1,1,8,256,256]{4,3,2,1,0:T(8,128)(2,1)} %val_hbm.1, s32[1,1,8,16,256]{4,3,2,1,0:T(8,128)} %mask_hbm.1, s32[1,1,8]{2,1,0:T(1,128)} %tc_ref.1), custom_call_target="tpu_custom_call" | custom-call | tf_op jit(solution)/shard_map/pallas_call | solution.py:269
  26.0 0.0 copy-start
  26.0 1.6 %copy.11 = f32[1,256,128]{2,1,0:T(8,128)} copy(f32[1,256,128]{2,1,0:T(8,128)} %get-tuple-element.12) | data formatting | bytes 262144
  27.6 0.0 copy-done
  27.6 0.6 %copy.12 = f32[1,128,128]{2,1,0:T(8,128)} copy(f32[1,128,128]{2,1,0:T(8,128)S(1)} %copy-done) | data formatting | bytes 131072
Async XLA Ops:
  26.0 1.6 %copy-start = (f32[1,128,128]{2,1,0:T(8,128)S(1)}, f32[1,128,128]{2,1,0:T(8,128)}, u32[]{:S(2)}) copy-start(f32[1,128,128]{2,1,0:T(8,128)} %get-tuple-element.13) | copy-start | bytes 196612

commit v2 on v1

--- a/solution.py
+++ b/solution.py
@@ -13,6 +13,7 @@
 NT = (((1,), (1,)), ((), ()))
 TN = (((0,), (0,)), ((), ()))
 WORD = 16
+CUTS = 2
 
 
 def loop(start, stop, body):
@@ -33,7 +34,7 @@
     nu_ref, nv_ref, loss_ref,
     uf, vf, vals, masks, ub, vb, keep, xsend, pbuf, rsend, rbuf,
     acc, vsend, vrecv, sq, lrow, lcol,
-    ld_sem, vg_s, vg_r, ug_s, ug_r, ud_s, ud_r, pd_s, pd_r, pr_s, pr_r,
+    ld_sem, vg_s, vg_r, up_s, dn_s, ug_r, ud_s, ud_r, pd_s, pd_r, pr_s, pr_r,
     vr_s, vr_r, lr_s, lr_r, lc_s, lc_r,
 ):
     n_q = n_c // 2
@@ -44,6 +45,7 @@
     pc = 2 * q + 1 - a
     tile = vals.shape[1]
     own_v = vf.shape[0]
+    part = tile // CUTS
     per_tile = tile // own_v
 
     ld_u = pltpu.make_async_copy(u_hbm.at[0], uf, ld_sem.at[0])
@@ -57,14 +59,16 @@
 
     bar = pltpu.get_barrier_semaphore()
 
-    def greet_row(d):
-        pl.semaphore_signal(bar, inc=1, device_id=((r + d) % n_r, c), device_id_type=MESH)
-
-    def greet_col(d):
-        pl.semaphore_signal(bar, inc=1, device_id=(r, (c + d) % n_c), device_id_type=MESH)
-
-    loop(1, n_r, greet_row)
-    loop(1, n_c, greet_col)
+    def greet(dev):
+        pl.semaphore_signal(bar, inc=1, device_id=dev, device_id_type=MESH)
+
+    def chain_greet():
+        greet((r, pc))
+        pl.when(q > 0)(lambda: greet((r, c - 2)))
+        pl.when(q < n_q - 1)(lambda: greet((r, c + 2)))
+
+    chain_greet()
+    loop(1, n_r, lambda d: greet(((r + d) % n_r, c)))
 
     ld_v.wait()
     vb[r // per_tile, pl.ds(pl.multiple_of((r % per_tile) * own_v, own_v), own_v)] = vf[...].astype(jnp.bfloat16)
@@ -74,7 +78,8 @@
     acc[...] = jnp.zeros_like(acc)
     penalty = fold(uf[...] * uf[...]) + fold(vf[...] * vf[...])
 
-    pl.semaphore_wait(bar, n_r + n_c - 2)
+    beside = (q + n_q - 1) // n_q + (2 * n_q - 2 - q) // n_q
+    pl.semaphore_wait(bar, n_r + beside)
 
     def chunk(i):
         return vb.at[i // per_tile, pl.ds(pl.multiple_of((i % per_tile) * own_v, own_v), own_v)]
@@ -91,29 +96,33 @@
         src = (r + n_r - d) % n_r
         return rdma(chunk(src), chunk(src), vg_s.at[d], vg_r.at[d], ((r + d) % n_r, c))
 
-    def chip(d):
-        return (q + n_q - d) % n_q
-
-    def ug(d):
-        return rdma(ub.at[c], ub.at[c], ug_s.at[d], ug_r.at[d], (r, 2 * ((q + d) % n_q) + a))
-
-    def ug_in(d):
-        s = 2 * chip(d) + a
-        return rdma(ub.at[s], ub.at[s], ug_s.at[d], ug_r.at[d], (r, 2 * ((q + d) % n_q) + a))
-
-    def ud(d):
-        s = 2 * chip(d) + a
-        return rdma(ub.at[s], ub.at[s], ud_s.at[d], ud_r.at[d], (r, pc))
-
-    def ud_in(d):
-        s = 2 * chip(d) + 1 - a
-        return rdma(ub.at[s], ub.at[s], ud_s.at[d], ud_r.at[d], (r, pc))
-
-    def pd(d):
-        return rdma(xsend.at[d], pbuf.at[d], pd_s.at[d], pd_r.at[d], (r, pc))
-
-    def pr(d):
-        return rdma(rsend.at[d], rbuf.at[d], pr_s.at[d], pr_r.at[d], (r, 2 * chip(d) + a))
+    def piece(s, k):
+        return ub.at[s, pl.ds(k * part, part)]
+
+    def up(t, k):
+        s = 2 * t + a
+        return rdma(piece(s, k), piece(s, k), up_s.at[t, k], ug_r.at[t, k], (r, c + 2))
+
+    def down(t, k):
+        s = 2 * t + a
+        return rdma(piece(s, k), piece(s, k), dn_s.at[t, k], ug_r.at[t, k], (r, c - 2))
+
+    def ud(t, k):
+        s = 2 * t + a
+        return rdma(piece(s, k), piece(s, k), ud_s.at[t, k], ud_r.at[t, k], (r, pc))
+
+    def ud_in(t, k):
+        s = 2 * t + 1 - a
+        return rdma(piece(s, k), piece(s, k), ud_s.at[t, k], ud_r.at[t, k], (r, pc))
+
+    def pd(t):
+        return rdma(xsend.at[t], pbuf.at[t], pd_s.at[t], pd_r.at[t], (r, pc))
+
+    def pr(t):
+        return rdma(rsend.at[t], rbuf.at[q], pr_s.at[t], pr_r.at[q], (r, 2 * t + a))
+
+    def pr_in(t):
+        return rdma(rsend.at[t], rbuf.at[t], pr_s.at[t], pr_r.at[t], (r, 2 * t + a))
 
     def vr(d):
         return rdma(vsend.at[(r + d) % n_r], vrecv.at[d], vr_s.at[d], vr_r.at[d], ((r + d) % n_r, c))
@@ -132,10 +141,30 @@
         src = (c + n_c - d) % n_c
         return rdma(lcol.at[src], lcol.at[src], lc_s.at[d], lc_r.at[d], (r, (c + d) % n_c))
 
+    def open_chain(k):
+        pl.when(q > 0)(lambda: down(q, k).start())
+        pl.when(q < n_q - 1)(lambda: up(q, k).start())
+        ud(q, k).start()
+
+    loop(0, CUTS, open_chain)
     loop(1, n_r, lambda d: vg(d).start())
-    ud(0).start()
-    loop(1, n_q, lambda d: ug(d).start())
-
+
+    def forward(h):
+        def below(k):
+            up(q - h, k).wait_recv()
+            pl.when(q < n_q - 1)(lambda: up(q - h, k).start())
+            ud(q - h, k).start()
+
+        def above(k):
+            down(q + h, k).wait_recv()
+            pl.when(q > 0)(lambda: down(q + h, k).start())
+            ud(q + h, k).start()
+
+        for k in range(CUTS):
+            pl.when(q >= h)(functools.partial(below, k))
+            pl.when(q + h < n_q)(functools.partial(above, k))
+
+    forward(1)
     ld_m.wait()
     ld_x.wait()
     loop(1, n_r, lambda d: vg_in(d).wait_recv())
@@ -157,40 +186,39 @@
         for t in range(acc.shape[0]):
             acc[t] += cols_t * (which == t).astype(jnp.float32)
 
-    def put_keep(d):
+    def put_keep(t):
         def put(x):
-            keep[d] = x
+            keep[t] = x
         return put
 
-    def put_send(d):
+    def put_send(t):
         def put(x):
-            xsend[d] = x.astype(jnp.bfloat16)
+            xsend[t] = x.astype(jnp.bfloat16)
         return put
 
-    def stage_c(d):
-        pd(d).wait_recv()
-        rsend[d] = (keep[d] + pbuf[d].astype(jnp.float32)).astype(jnp.bfloat16)
-        pr(d).start()
-
-    def stage_a(d):
-        ug_in(d).wait_recv()
-        ud(d).start()
-        slot(2 * chip(d) + a, put_keep(d))
-
-    def stage_b(d):
-        ud_in(d).wait_recv()
-        slot(2 * chip(d) + 1 - a, put_send(d))
-        pd(d).start()
-
-    slot(c, put_keep(0))
-    stage_b(0)
-    stage_a(1)
-    stage_b(1)
-
-    def step(d):
-        stage_a(d)
-        stage_c(d - 1)
-        stage_b(d)
+    def both(t):
+        slot(2 * t + a, put_keep(t))
+        for k in range(CUTS):
+            ud_in(t, k).wait_recv()
+        slot(2 * t + 1 - a, put_send(t))
+        pd(t).start()
+
+    def pass_on(t):
+        pd(t).wait_recv()
+        rsend[t] = (keep[t] + pbuf[t].astype(jnp.float32)).astype(jnp.bfloat16)
+        pr(t).start()
+
+    def sides(h, what):
+        pl.when(q >= h)(lambda: what(q - h))
+        pl.when(q + h < n_q)(lambda: what(q + h))
+
+    both(q)
+    sides(1, both)
+
+    def step(h):
+        forward(h)
+        sides(h - 1, pass_on)
+        sides(h, both)
 
     loop(2, n_q, step)
 
@@ -203,15 +231,15 @@
             vsend[t * per_tile + h] = whole[h * own_v:(h + 1) * own_v]
     loop(1, n_r, lambda d: lr(d).start())
     loop(1, n_r, lambda d: vr(d).start())
-    stage_c(n_q - 1)
+    sides(n_q - 1, pass_on)
 
     loop(1, n_r, lambda d: lr_in(d).wait_recv())
     total = lrow[0]
     for i in range(1, n_r):
         total = total + lrow[i]
     lcol[c] = total
-    pd(0).wait_recv()
-    keep[0] = keep[0] + pbuf[0].astype(jnp.float32)
+    pd(q).wait_recv()
+    keep[q] = keep[q] + pbuf[q].astype(jnp.float32)
     loop(1, n_c, lambda d: lc(d).start())
 
     def add_v(d):
@@ -224,11 +252,12 @@
     vf_sum[...] = vf[...] - step_rate * (vf_sum[...] + ridge_weight * vf[...])
 
     def add_u(d):
-        pr(d).wait_recv()
-        keep[0] += rbuf[d].astype(jnp.float32)
+        t = (q + d) % n_q
+        pr_in(t).wait_recv()
+        keep[q] += rbuf[t].astype(jnp.float32)
 
     loop(1, n_q, add_u)
-    nu_ref[0] = uf[...] - step_rate * (keep[0] + ridge_weight * uf[...])
+    nu_ref[0] = uf[...] - step_rate * (keep[q] + ridge_weight * uf[...])
 
     loop(1, n_c, lambda d: lc_in(d).wait_recv())
     total = lcol[0]
@@ -236,13 +265,15 @@
         total = total + lcol[i]
     loss_ref[...] = jnp.sum(jnp.sum(total, axis=1, keepdims=True), axis=0, keepdims=True) / entries
 
-    def drain_q(d):
-        ud(d).wait_send()
-        pd(d).wait_send()
+    def drain_q(t):
+        pd(t).wait_send()
+        for k in range(CUTS):
+            ud(t, k).wait_send()
+            pl.when(jnp.logical_and(t <= q, q < n_q - 1))(lambda: up(t, k).wait_send())
+            pl.when(jnp.logical_and(t >= q, q > 0))(lambda: down(t, k).wait_send())
 
     def drain_q1(d):
-        ug(d).wait_send()
-        pr(d).wait_send()
+        pr((q + d) % n_q).wait_send()
 
     def drain_r(d):
         vg(d).wait_send()
@@ -269,8 +300,8 @@
     new_u, new_v, loss = pl.pallas_call(
         functools.partial(kernel, n_r, n_c, float(entries)),
         out_shape=(
-            jax.ShapeDtypeStruct(factor_u.shape, f32),
-            jax.ShapeDtypeStruct(factor_v.shape, f32),
+            pltpu.VMEM(factor_u.shape, f32),
+            pltpu.VMEM(factor_v.shape, f32),
             jax.ShapeDtypeStruct((1, 1), f32),
         ),
         in_specs=[anym, anym, anym, anym, pl.BlockSpec(memory_space=pltpu.SMEM)],
@@ -295,8 +326,8 @@
             pltpu.VMEM((n_c, 8, tile // 2), f32),
             dma((4,)),
             dma((n_r,)), dma((n_r,)),
-            dma((n_q,)), dma((n_q,)),
-            dma((n_q,)), dma((n_q,)),
+            dma((n_q, CUTS)), dma((n_q, CUTS)), dma((n_q, CUTS)),
+            dma((n_q, CUTS)), dma((n_q, CUTS)),
             dma((n_q,)), dma((n_q,)),
             dma((n_q,)), dma((n_q,)),
             dma((n_r,)), dma((n_r,)),

time: 30.1 us -> 27.9 us (0.927)
  Pallas kernels: 25.4 us -> 24.1 us
  local copies, waits for them, and re-layouts: 2.23 us -> 1.29 us
    pallas_call x1, Pallas kernels: 25.4 us -> 24.1 us  [per_device(): pl.pallas_call(functools.partial(kernel, n_r, n_c, float(entries)), out_s...]
    unnamed x4 -> x2, local copies, waits for them, and re-layouts: 2.23 us -> 1.29 us
where the time goes in v2:
time: 27.9 us; the launch traced here: 27.7 us
  Pallas kernels  24.1 us (86%)
  between operations  2.33 us (8%)
  local copies, waits for them, and re-layouts  1.29 us (5%)
    pallas_call x1, Pallas kernels, per_device(): pl.pallas_call(functools.partial(kernel, n_r, n_c, float(entries)), out_s...  24.1 us
    unnamed x2, local copies, waits for them, and re-layouts  1.29 us

profile of v2, /device:TPU:0, one launch (start us, length us, event | category | flops | bytes accessed | tf_op | source)
XLA Modules:
  0.0 27.7 jit_solution(9190393252548780415)
XLA Ops:
  0.6 24.1 %shard_map.76 = (f32[1,256,128]{2,1,0:T(8,128)S(1)}, f32[1,128,128]{2,1,0:T(8,128)S(1)}, f32[1,1]{1,0:T(1,128)}) custom-call(f32[1,256,128]{2,1,0:T(8,128)} %u_hbm.1, f32[1,128,128]{2,1,0:T(8,128)} %v_hbm.1, bf16[1,1,8,256,256]{4,3,2,1,0:T(8,128)(2,1)} %val_hbm.1, s32[1,1,8,16,256]{4,3,2,1,0:T(8,128)} %mask_hbm.1, s32[1,1,8]{2,1,0:T(1,128)} %tc_ref.1), custom_call_target="tpu_custom_call" | custom-call | tf_op jit(solution)/shard_map/pallas_call | solution.py:300
  24.8 0.7 %copy.11 = f32[1,256,128]{2,1,0:T(8,128)} copy(f32[1,256,128]{2,1,0:T(8,128)S(1)} %get-tuple-element.9) | data formatting | bytes 262144
  25.4 0.6 %copy.12 = f32[1,128,128]{2,1,0:T(8,128)} copy(f32[1,128,128]{2,1,0:T(8,128)S(1)} %get-tuple-element.10) | data formatting | bytes 131072

commit v3 on v2

--- a/solution.py
+++ b/solution.py
@@ -225,11 +225,14 @@
     half = sq.shape[1] // 2
     lrow[r] = 0.5 * (sq[:, :half] + sq[:, half:]) + 0.5 * ridge_weight * penalty
 
-    for t in range(acc.shape[0]):
+    def finish_tile(t):
         whole = acc[t].T.astype(jnp.bfloat16)
         for h in range(per_tile):
             vsend[t * per_tile + h] = whole[h * own_v:(h + 1) * own_v]
+
+    finish_tile(0)
     loop(1, n_r, lambda d: lr(d).start())
+    loop(1, acc.shape[0], finish_tile)
     loop(1, n_r, lambda d: vr(d).start())
     sides(n_q - 1, pass_on)
 
@@ -302,7 +305,7 @@
         out_shape=(
             pltpu.VMEM(factor_u.shape, f32),
             pltpu.VMEM(factor_v.shape, f32),
-            jax.ShapeDtypeStruct((1, 1), f32),
+            pltpu.VMEM((1, 1), f32),
         ),
         in_specs=[anym, anym, anym, anym, pl.BlockSpec(memory_space=pltpu.SMEM)],
         out_specs=(vm, vm, vm),

time: 27.9 us -> 26.9 us (0.964)
  between operations: 2.33 us -> 1.8 us
  Pallas kernels: 24.1 us -> 23.7 us
    pallas_call x1, Pallas kernels: 24.1 us -> 23.7 us  [per_device(): pl.pallas_call(functools.partial(kernel, n_r, n_c, float(entries)), out_s...]
where the time goes in v3:
time: 26.9 us; the launch traced here: 26.8 us
  Pallas kernels  23.7 us (88%)
  between operations  1.8 us (7%)
  local copies, waits for them, and re-layouts  1.29 us (5%)
    pallas_call x1, Pallas kernels, per_device(): pl.pallas_call(functools.partial(kernel, n_r, n_c, float(entries)), out_s...  23.7 us
    unnamed x2, local copies, waits for them, and re-layouts  1.29 us

profile of v3, /device:TPU:0, one launch (start us, length us, event | category | flops | bytes accessed | tf_op | source)
XLA Modules:
  0.0 26.8 jit_solution(5510574839093809149)
XLA Ops:
  0.6 23.7 %shard_map.76 = (f32[1,256,128]{2,1,0:T(8,128)S(1)}, f32[1,128,128]{2,1,0:T(8,128)S(1)}, f32[1,1]{1,0:T(1,128)S(1)}) custom-call(f32[1,256,128]{2,1,0:T(8,128)} %u_hbm.1, f32[1,128,128]{2,1,0:T(8,128)} %v_hbm.1, bf16[1,1,8,256,256]{4,3,2,1,0:T(8,128)(2,1)} %val_hbm.1, s32[1,1,8,16,256]{4,3,2,1,0:T(8,128)} %mask_hbm.1, s32[1,1,8]{2,1,0:T(1,128)} %tc_ref.1), custom_call_target="tpu_custom_call" | custom-call | tf_op jit(solution)/shard_map/pallas_call | solution.py:303
  24.4 0.7 %copy.11 = f32[1,256,128]{2,1,0:T(8,128)} copy(f32[1,256,128]{2,1,0:T(8,128)S(1)} %get-tuple-element.9) | data formatting | bytes 262144
  25.0 0.6 %copy.12 = f32[1,128,128]{2,1,0:T(8,128)} copy(f32[1,128,128]{2,1,0:T(8,128)S(1)} %get-tuple-element.10) | data formatting | bytes 131072
